TPU v7x, 32 devices: a whole 2x2x4 slice. The times are simulated.
32 devices in a mesh: job: 2 (over y), ta: 4 (over z), xyz: 2 (over x), src: 2 (over core).
Axes of the slice: x: 2, y: 2, z: 4, core: 2. Of those that a mesh axis runs over, the one named last changes fastest.
Arguments:
- spinors: float32 [64, 8, 2, 8, 3, 512], P('src', 'ta', None, 'job', None, 'xyz'), parts along dimension 3, may hold values from -6 to 6
- eigvecs: float32 [8, 256, 2, 3, 512], P('ta', 'job', None, None, 'xyz'), parts along dimension 1, may hold values from -0.109375 to 0.109375
- group_of: int32 [8], replicated, may hold values from 0 to 3, as said below
- source_ids: int32 [64], P('src'), may hold values from 0 to 63, as said below
Outputs:
- perambulator: float32 [8, 2, 8, 64, 128], P('ta', None, 'job', 'src', 'xyz'), parts along dimension 2
There are 2 independent parts, one for each index of `job`. A program takes and returns all parts, laid end to end along the dimension named above; an argument that names none is the same for every part. Nothing has to cross between parts.
Inputs may be any that keep to these rules, and one draw needn't show every extreme that they name: `group_of`: every group number appears exactly 2 times. `source_ids`: the 32 entries held by index i of src are a permutation of i * 32 to (i + 1) * 32 - 1.
All inputs are finite; a program needn't handle non-finite values.
Results may differ from a plain program's by a relative error of at most 0.00007.
Values sent between devices are 32-bit elements; how exact they have to be, the bound alone decides.
A program may use at most 64 MiB of HBM per device.

v0:
```python
import jax
import jax.numpy as jnp
from jax import lax
from jax.sharding import PartitionSpec as P


def contract_pair(vectors, spinor):
    vector_real = vectors[:, :, 0]
    vector_imag = vectors[:, :, 1]
    spinor_real = spinor[:, :, 0]
    spinor_imag = spinor[:, :, 1]

    def contract(left_side, right_side):
        return jnp.einsum(
            "tkcx,ntscx->tsnk", left_side, right_side, precision=lax.Precision.HIGHEST
        )

    real_part = contract(vector_real, spinor_real) + contract(vector_imag, spinor_imag)
    imag_part = contract(vector_real, spinor_imag) - contract(vector_imag, spinor_real)
    return jnp.stack([real_part, imag_part], axis=1)


def local(spinors, eigvecs, group_of, source_ids):
    extent = group_of.shape[0]
    sort_keys = group_of * extent + jnp.arange(extent, dtype=jnp.int32)
    ordering = jnp.argsort(sort_keys)
    spread = lax.all_to_all(spinors, "ta", split_axis=0, concat_axis=1, tiled=True)
    grouped = jnp.take(spread, ordering, axis=1)
    regrouped = lax.all_to_all(grouped, "ta", split_axis=1, concat_axis=0, tiled=True)
    partial_sums = contract_pair(eigvecs, regrouped)
    summed = lax.psum_scatter(partial_sums, "xyz", scatter_dimension=4, tiled=True)
    inverse = jnp.argsort(source_ids)
    return jnp.take(summed, inverse, axis=3)


def solution(mesh):
    in_specs = (
        P("src", "ta", None, "job", None, "xyz"),
        P("ta", "job", None, None, "xyz"),
        P(),
        P("src"),
    )
    out_specs = P("ta", None, "job", "src", "xyz")
    return jax.shard_map(local, mesh=mesh, in_specs=in_specs, out_specs=out_specs, check_vma=False)
```

profile of v0, /device:TPU:0, one launch (start us, length us, event | category | flops | bytes accessed | tf_op | source)
XLA Modules:
  0.0 120.4 jit_solution(10331369571114613765)
XLA Ops:
  6.5 0.0 copy-start
  6.5 6.5 %all-to-all-start = ((f32[32,2,2,4,3,256]{5,3,4,2,1,0:T(4,128)}), f32[32,2,2,4,3,256]{5,3,4,2,1,0:T(4,128)S(1)}, u32[]{:S(2)}, u32[]{:S(2)}) async-start(f32[32,2,2,4,3,256]{5,3,4,2,1,0:T(4,128)} %param.4), calls=%async_computation | async-start | bytes 3145728 | tf_op jit(solution)/shard_map/all_to_all | solution.py:27
  13.0 0.0 copy-done
  13.0 1.0 sort.35
  14.0 36.0 %all-to-all-done = f32[32,2,2,4,3,256]{5,3,4,2,1,0:T(4,128)S(1)} async-done(((f32[32,2,2,4,3,256]{5,3,4,2,1,0:T(4,128)}), f32[32,2,2,4,3,256]{5,3,4,2,1,0:T(4,128)S(1)}, u32[]{:S(2)}, u32[]{:S(2)}) %all-to-all-start) | async-done | bytes 1572896 | tf_op jit(solution)/shard_map/all_to_all | solution.py:27
  50.0 0.9 copy.55
  50.9 0.2 copy.29
  51.1 0.7 gather_fusion
  51.7 1.4 %select_bitcast_fusion = f32[8,8,2,4,3,256]{5,0,4,3,2,1:T(8,128)} fusion(f32[8,8,2,4,3,256]{5,1,4,3,2,0:T(8,128)S(1)} %gather_fusion, pred[8]{0:T(512)(128)(4,1)S(1)} %compare_and_fusion), kind=kLoop, calls=%fused_computation.4 | loop fusion | flops 393216 | bytes 3145736 | tf_op jit(solution)/shard_map/jit(_take)/select_n | solution.py:28
  53.1 0.0 copy-start.1
  53.2 3.7 %all-to-all-start.1 = ((f32[8,8,2,4,3,256]{5,0,4,3,2,1:T(8,128)}), f32[8,8,2,4,3,256]{5,0,4,3,2,1:T(8,128)S(1)}, u32[]{:S(2)}, u32[]{:S(2)}) async-start(f32[8,8,2,4,3,256]{5,0,4,3,2,1:T(8,128)} %select_bitcast_fusion), calls=%async_computation.1 | async-start | bytes 3145728 | tf_op jit(solution)/shard_map/all_to_all | solution.py:29
  56.9 0.0 reduce-scatter.4.cloned.1.call-start
  56.9 0.0 copy-done.1
  56.9 1.6 %sort.34 = (s32[32]{0:T(128)}, s32[32]{0:T(128)S(1)}) sort(s32[32]{0:T(128)S(1)} %copy-done.1, s32[32]{0:T(128)S(1)} %iota.11), dimensions={0}, to_apply=%region_0.0 | sort | flops 160 | bytes 512 | tf_op jit(solution)/shard_map/jit(argsort)/sort | solution.py:32
  58.5 3.4 %fusion.4 = (f32[2,128,1,3,256]{4,2,3,1,0:T(1,128)S(1)}, f32[2,128,1,3,256]{4,2,3,1,0:T(1,128)S(1)}) fusion(f32[2,128,2,3,256]{4,2,3,1,0:T(2,128)} %param.5), kind=kLoop, calls=%fused_computation.26 | loop fusion | bytes 3145728 | tf_op jit(solution)/shard_map/slice | solution.py:8
  61.9 31.4 %all-to-all-done.1 = f32[8,8,2,4,3,256]{5,0,4,3,2,1:T(8,128)S(1)} async-done(((f32[8,8,2,4,3,256]{5,0,4,3,2,1:T(8,128)}), f32[8,8,2,4,3,256]{5,0,4,3,2,1:T(8,128)S(1)}, u32[]{:S(2)}, u32[]{:S(2)}) %all-to-all-start.1) | async-done | bytes 1572896 | tf_op jit(solution)/shard_map/all_to_all | solution.py:29
  93.3 0.2 copy.54
  93.6 0.9 convolution_bitcast_fusion.2
  94.5 0.9 convolution_bitcast_fusion
  95.3 0.9 fusion.1
  96.2 0.9 fusion.3
  97.1 0.6 copy.41
  97.7 1.7 %reshape.34 = f32[128,512]{1,0:T(8,128)} reshape(f32[128,2,2,4,32]{4,3,2,1,0:T(4,128)S(1)} %bitcast.76) | data formatting | bytes 524288
  99.4 0.0 reduce-scatter.4.cloned.1.call-update
  99.5 11.0 %reduce-scatter.4.cloned.1.call-done = f32[64,512]{1,0:T(8,128)} async-done(((f32[128,512]{1,0:T(8,128)}), f32[64,512]{1,0:T(8,128)}) %reduce-scatter.4.cloned.1.call-update) | async-done | bytes 131088
  110.4 1.2 reshape.35
  111.6 0.3 copy.33
  111.9 0.7 gather_fusion.1
  112.7 0.1 select_bitcast_fusion.1
  112.8 0.8 copy.34
  (10 shorter events, 0.1 us)
Async XLA Ops:
  6.5 6.5 %copy-start = (s32[8]{0:T(128)S(1)}, s32[8]{0:T(128)}, u32[]{:S(2)}) copy-start(s32[8]{0:T(128)} %param.6) | copy-start | bytes 100
  6.5 43.4 %all-to-all-start = ((f32[32,2,2,4,3,256]{5,3,4,2,1,0:T(4,128)}), f32[32,2,2,4,3,256]{5,3,4,2,1,0:T(4,128)S(1)}, u32[]{:S(2)}, u32[]{:S(2)}) async-start(f32[32,2,2,4,3,256]{5,3,4,2,1,0:T(4,128)} %param.4), calls=%async_computation | async-start | bytes 3145728 | tf_op jit(solution)/shard_map/all_to_all | solution.py:27
  53.1 3.8 %copy-start.1 = (s32[32]{0:T(128)S(1)}, s32[32]{0:T(128)}, u32[]{:S(2)}) copy-start(s32[32]{0:T(128)} %param.7) | copy-start | bytes 388
  53.2 40.2 %all-to-all-start.1 = ((f32[8,8,2,4,3,256]{5,0,4,3,2,1:T(8,128)}), f32[8,8,2,4,3,256]{5,0,4,3,2,1:T(8,128)S(1)}, u32[]{:S(2)}, u32[]{:S(2)}) async-start(f32[8,8,2,4,3,256]{5,0,4,3,2,1:T(8,128)} %select_bitcast_fusion), calls=%async_computation.1 | async-start | bytes 3145728 | tf_op jit(solution)/shard_map/all_to_all | solution.py:29
  56.9 53.6 %reduce-scatter.4.cloned.1.call-start = ((), (), s32[]{:S(2)}) async-start(), calls=%async_computation.3 | async-start | bytes 393216
Sparse Core Ops, SparseCore 0:
  99.5 10.8 reduce-scatter.3
where the time goes:
time: 121 us; the launch traced here: 120 us
  waiting for transfers between devices  78.4 us (65%)
  between operations  13.6 us (11%)
  local copies, waits for them, and re-layouts  10.6 us (9%)
  starting transfers between devices  10.2 us (8%)
  other arithmetic  4.16 us (3%)
  matrix products  3.51 us (3%)
    all_to_all x1, waiting for transfers between devices, local(): lax.all_to_all(spinors, 'ta', split_axis=0, concat_axis=1, tiled=True)  36 us
    all_to_all x1, waiting for transfers between devices, local(): lax.all_to_all(grouped, 'ta', split_axis=1, concat_axis=0, tiled=True)  31.4 us
    unnamed x2, waiting for transfers between devices  11 us
    all_to_all x1, starting transfers between devices, local(): lax.all_to_all(spinors, 'ta', split_axis=0, concat_axis=1, tiled=True)  6.48 us
    all_to_all x1, starting transfers between devices, local(): lax.all_to_all(grouped, 'ta', split_axis=1, concat_axis=0, tiled=True)  3.69 us
    dot_general x4, matrix products, contract(): jnp.einsum('tkcx,ntscx->tsnk', left_side, right_side, precision=lax.Preci...  3.51 us
    unnamed x7, local copies, waits for them, and re-layouts  3.43 us
    slice x1, local copies, waits for them, and re-layouts, contract_pair(): vector_real = vectors[:, :, 0]  3.37 us
  transfers between devices with their start and end apart: 3, of which 3 were waited for; matrix products, arithmetic and copies ran while one was open for 5% of the time, Pallas kernels for 0%

commit v1 on v0

--- a/solution.py
+++ b/solution.py
@@ -26,7 +26,19 @@
     ordering = jnp.argsort(sort_keys)
     spread = lax.all_to_all(spinors, "ta", split_axis=0, concat_axis=1, tiled=True)
     grouped = jnp.take(spread, ordering, axis=1)
-    regrouped = lax.all_to_all(grouped, "ta", split_axis=1, concat_axis=0, tiled=True)
+    ways, here = (lax.axis_size("ta"), lax.axis_index("ta"))
+    width = grouped.shape[1] // ways
+    shape = list(grouped.shape)
+    shape[1] = width
+    height = shape[0]
+    shape[0] = height * ways
+    full = jnp.zeros(shape, grouped.dtype)
+    for mask in range(ways):
+        part = lax.dynamic_slice_in_dim(grouped, (here ^ mask) * width, width, axis=1)
+        if mask:
+            part = lax.ppermute(part, "ta", [(d, d ^ mask) for d in range(ways)])
+        full = lax.dynamic_update_slice_in_dim(full, part, (here ^ mask) * height, axis=0)
+    regrouped = full
     partial_sums = contract_pair(eigvecs, regrouped)
     summed = lax.psum_scatter(partial_sums, "xyz", scatter_dimension=4, tiled=True)
     inverse = jnp.argsort(source_ids)

time: 121 us -> 115 us (0.950)
  waiting for transfers between devices: 78.4 us -> 72.9 us
    all_to_all x1 -> x0, waiting for transfers between devices: 31.4 us -> none  [local(): lax.all_to_all(grouped, 'ta', split_axis=1, concat_axis=0, tiled=True)]
    ppermute x0 -> x3, waiting for transfers between devices: none -> 20.3 us  [local(): part = lax.ppermute(part, 'ta', [(d, d ^ mask) for d in range(ways)])]
    unnamed x2, waiting for transfers between devices: 11 us -> 16.7 us
    ppermute x0 -> x3, starting transfers between devices: none -> 4.44 us  [local(): part = lax.ppermute(part, 'ta', [(d, d ^ mask) for d in range(ways)])]
    all_to_all x1 -> x0, starting transfers between devices: 3.69 us -> none  [local(): lax.all_to_all(grouped, 'ta', split_axis=1, concat_axis=0, tiled=True)]
    dynamic_update_slice x0 -> x4, local copies, waits for them, and re-layouts: none -> 2.17 us  [local(): lax.dynamic_update_slice_in_dim(full, part, (here ^ mask) * height, axis=0)]
    slice x1, local copies, waits for them, and re-layouts: 3.37 us -> 1.21 us  [contract_pair(): vector_real = vectors[:, :, 0]]
    unnamed x7 -> x11, local copies, waits for them, and re-layouts: 3.43 us -> 3.44 us
  transfers between devices with their start and end apart: 3 -> 5, of which waited for: 3 -> 4; matrix products, arithmetic and copies ran while one was open for 5% -> 5% of each run, Pallas kernels for 0% -> 0%
where the time goes in v1:
time: 115 us
  waiting for transfers between devices  72.9 us (63%)
  between operations  13.6 us (12%)
  starting transfers between devices  10.9 us (9%)
  local copies, waits for them, and re-layouts  10.7 us (9%)
  matrix products  3.51 us (3%)
  other arithmetic  2.99 us (3%)
    all_to_all x1, waiting for transfers between devices, local(): lax.all_to_all(spinors, 'ta', split_axis=0, concat_axis=1, tiled=True)  36 us
    ppermute x3, waiting for transfers between devices, local(): part = lax.ppermute(part, 'ta', [(d, d ^ mask) for d in range(ways)])  20.3 us
    unnamed x2, waiting for transfers between devices  16.7 us
    all_to_all x1, starting transfers between devices, local(): lax.all_to_all(spinors, 'ta', split_axis=0, concat_axis=1, tiled=True)  6.48 us
    ppermute x3, starting transfers between devices, local(): part = lax.ppermute(part, 'ta', [(d, d ^ mask) for d in range(ways)])  4.44 us
    dot_general x4, matrix products, contract(): jnp.einsum('tkcx,ntscx->tsnk', left_side, right_side, precision=lax.Preci...  3.51 us
    unnamed x11, local copies, waits for them, and re-layouts  3.44 us
  transfers between devices with their start and end apart: 5, of which 4 were waited for; matrix products, arithmetic and copies ran while one was open for 5% of the time, Pallas kernels for 0%

profile of v1, /device:TPU:0, one launch (start us, length us, event | category | flops | bytes accessed | tf_op | source)
XLA Modules:
  0.0 114.7 jit_solution(5272722936706682597)
XLA Ops:
  6.5 0.0 copy-start.2
  6.5 6.5 %all-to-all-start = ((f32[32,2,2,4,3,256]{5,3,4,2,1,0:T(4,128)}), f32[32,2,2,4,3,256]{5,3,4,2,1,0:T(4,128)S(1)}, u32[]{:S(2)}, u32[]{:S(2)}) async-start(f32[32,2,2,4,3,256]{5,3,4,2,1,0:T(4,128)} %param.4), calls=%async_computation | async-start | bytes 3145728 | tf_op jit(solution)/shard_map/all_to_all | solution.py:27
  13.0 0.0 reduce-scatter.4.cloned.1.call-start
  13.0 0.0 copy-done.2
  13.0 1.0 sort.35
  14.0 36.0 %all-to-all-done = f32[32,2,2,4,3,256]{5,3,4,2,1,0:T(4,128)S(1)} async-done(((f32[32,2,2,4,3,256]{5,3,4,2,1,0:T(4,128)}), f32[32,2,2,4,3,256]{5,3,4,2,1,0:T(4,128)S(1)}, u32[]{:S(2)}, u32[]{:S(2)}) %all-to-all-start) | async-done | bytes 1572896 | tf_op jit(solution)/shard_map/all_to_all | solution.py:27
  50.0 0.9 copy.54
  50.9 0.2 copy.29
  51.1 0.7 gather_fusion
  51.7 0.2 copy_select_fusion
  52.0 0.0 copy-start
  52.0 0.0 copy-start.1
  52.0 0.1 dynamic-slice_bitcast_fusion
  52.1 0.1 collective-permute-start
  52.2 2.0 %collective-permute-start.1 = (f32[8,2,2,4,3,256]{5,0,4,3,1,2:T(8,128)S(1)}, f32[8,2,2,4,3,256]{5,0,4,3,1,2:T(8,128)S(1)}, u32[]{:S(2)}, u32[]{:S(2)}) collective-permute-start(f32[8,2,2,4,3,256]{5,0,4,3,1,2:T(8,128)S(1)} %get-tuple-element.12), channel_id=1, source_target_pairs={{0,8},{4,12},{8,0},{12,4},{1,9},{5,13},{9,1},{13,5},{2,10},{6,14},... | collective-permute-start | bytes 1179656 | tf_op jit(solution)/shard_map/ppermute | solution.py:39
  54.2 0.0 copy-done
  54.2 0.0 copy-start.3
  54.2 2.4 %collective-permute-start.2 = (f32[8,2,2,4,3,256]{5,0,4,3,1,2:T(8,128)S(1)}, f32[8,2,2,4,3,256]{5,0,4,3,1,2:T(8,128)S(1)}, u32[]{:S(2)}, u32[]{:S(2)}) collective-permute-start(f32[8,2,2,4,3,256]{5,0,4,3,1,2:T(8,128)S(1)} %get-tuple-element.11), channel_id=1, source_target_pairs={{0,12},{4,8},{8,4},{12,0},{1,13},{5,9},{9,5},{13,1},{2,14},{6,10},... | collective-permute-start | bytes 1179656 | tf_op jit(solution)/shard_map/ppermute | solution.py:39
  56.6 0.0 copy-done.1
  56.6 1.2 %fusion.4 = (f32[2,128,1,3,256]{4,2,3,1,0:T(1,128)S(1)}, f32[2,128,1,3,256]{4,2,3,1,0:T(1,128)S(1)}) fusion(f32[2,128,2,3,256]{4,2,3,1,0:T(2,128)S(1)} %copy-done.1), kind=kLoop, calls=%fused_computation.32 | loop fusion | bytes 3145728 | tf_op jit(solution)/shard_map/slice | solution.py:8
  57.8 0.0 copy-done.3
  57.8 1.6 %sort.34 = (s32[32]{0:T(128)}, s32[32]{0:T(128)S(1)}) sort(s32[32]{0:T(128)S(1)} %copy-done.3, s32[32]{0:T(128)S(1)} %iota.11), dimensions={0}, to_apply=%region_0.0 | sort | flops 160 | bytes 512 | tf_op jit(solution)/shard_map/jit(argsort)/sort | solution.py:44
  59.5 0.2 broadcast_in_dim.28
  59.6 1.0 bitcast_dynamic-update-slice_fusion
  60.7 9.3 %collective-permute-done = f32[8,2,2,4,3,256]{5,0,4,3,1,2:T(8,128)} collective-permute-done((f32[8,2,2,4,3,256]{5,0,4,3,1,2:T(8,128)S(1)}, f32[8,2,2,4,3,256]{5,0,4,3,1,2:T(8,128)}, u32[]{:S(2)}, u32[]{:S(2)}) %collective-permute-start) | collective-permute-done | bytes 393248 | tf_op jit(solution)/shard_map/ppermute | solution.py:39
  70.0 1.0 constant_dynamic-update-slice_fusion.1
  71.1 11.0 %collective-permute-done.1 = f32[8,2,2,4,3,256]{5,0,4,3,1,2:T(8,128)S(1)} collective-permute-done((f32[8,2,2,4,3,256]{5,0,4,3,1,2:T(8,128)S(1)}, f32[8,2,2,4,3,256]{5,0,4,3,1,2:T(8,128)S(1)}, u32[]{:S(2)}, u32[]{:S(2)}) %collective-permute-start.1) | collective-permute-done | bytes 393248 | tf_op jit(solution)/shard_map/ppermute | solution.py:39
  82.1 0.0 collective-permute-done.2
  82.1 0.9 convolution_bitcast_fusion.2
  83.0 0.9 convolution_bitcast_fusion
  83.9 0.9 fusion.1
  84.8 0.9 fusion.3
  85.7 0.6 copy.41
  86.3 1.7 %reshape.34 = f32[128,512]{1,0:T(8,128)} reshape(f32[128,2,2,4,32]{4,3,2,1,0:T(4,128)S(1)} %bitcast.71) | data formatting | bytes 524288
  88.0 0.0 reduce-scatter.4.cloned.1.call-update
  88.0 16.6 %reduce-scatter.4.cloned.1.call-done = f32[64,512]{1,0:T(8,128)} async-done(((f32[128,512]{1,0:T(8,128)}), f32[64,512]{1,0:T(8,128)}) %reduce-scatter.4.cloned.1.call-update) | async-done | bytes 131088
  104.7 1.2 %reshape.35 = f32[64,2,2,4,32]{4,3,2,1,0:T(4,128)S(1)} reshape(f32[64,512]{1,0:T(8,128)} %reduce-scatter.4.cloned.1.call-done) | data formatting | bytes 262144
  105.8 0.3 copy.33
  106.2 0.7 gather_fusion.1
  106.9 0.1 select_bitcast_fusion
  107.0 0.8 copy.34
  (12 shorter events, 0.1 us)
Async XLA Ops:
  6.5 6.5 %copy-start.2 = (s32[8]{0:T(128)S(1)}, s32[8]{0:T(128)}, u32[]{:S(2)}) copy-start(s32[8]{0:T(128)} %param.6) | copy-start | bytes 100
  6.5 43.4 %all-to-all-start = ((f32[32,2,2,4,3,256]{5,3,4,2,1,0:T(4,128)}), f32[32,2,2,4,3,256]{5,3,4,2,1,0:T(4,128)S(1)}, u32[]{:S(2)}, u32[]{:S(2)}) async-start(f32[32,2,2,4,3,256]{5,3,4,2,1,0:T(4,128)} %param.4), calls=%async_computation | async-start | bytes 3145728 | tf_op jit(solution)/shard_map/all_to_all | solution.py:27
  13.0 91.7 %reduce-scatter.4.cloned.1.call-start = ((), (), s32[]{:S(2)}) async-start(), calls=%async_computation.2 | async-start | bytes 393216
  52.0 2.2 %copy-start = (f32[8,8,2,4,3,256]{5,1,4,3,0,2:T(8,128)}, f32[8,8,2,4,3,256]{5,1,4,3,0,2:T(8,128)S(1)}, u32[]{:S(2)}) copy-start(f32[8,8,2,4,3,256]{5,1,4,3,0,2:T(8,128)S(1)} %copy_select_fusion) | copy-start | bytes 4718596
  52.0 4.6 %copy-start.1 = (f32[2,128,2,3,256]{4,2,3,1,0:T(2,128)S(1)}, f32[2,128,2,3,256]{4,2,3,1,0:T(2,128)}, u32[]{:S(2)}) copy-start(f32[2,128,2,3,256]{4,2,3,1,0:T(2,128)} %param.5) | copy-start | bytes 4718596
  52.1 17.9 %collective-permute-start = (f32[8,2,2,4,3,256]{5,0,4,3,1,2:T(8,128)S(1)}, f32[8,2,2,4,3,256]{5,0,4,3,1,2:T(8,128)}, u32[]{:S(2)}, u32[]{:S(2)}) collective-permute-start(f32[8,2,2,4,3,256]{5,0,4,3,1,2:T(8,128)S(1)} %get-tuple-element.13), channel_id=1, source_target_pairs={{0,4},{4,0},{8,12},{12,8},{1,5},{5,1},{9,13},{13,9},{2,6},{6,2},{1... | collective-permute-start | bytes 1179656 | tf_op jit(solution)/shard_map/ppermute | solution.py:39
  52.2 29.8 %collective-permute-start.1 = (f32[8,2,2,4,3,256]{5,0,4,3,1,2:T(8,128)S(1)}, f32[8,2,2,4,3,256]{5,0,4,3,1,2:T(8,128)S(1)}, u32[]{:S(2)}, u32[]{:S(2)}) collective-permute-start(f32[8,2,2,4,3,256]{5,0,4,3,1,2:T(8,128)S(1)} %get-tuple-element.12), channel_id=1, source_target_pairs={{0,8},{4,12},{8,0},{12,4},{1,9},{5,13},{9,1},{13,5},{2,10},{6,14},... | collective-permute-start | bytes 1179656 | tf_op jit(solution)/shard_map/ppermute | solution.py:39
  54.2 3.6 %copy-start.3 = (s32[32]{0:T(128)S(1)}, s32[32]{0:T(128)}, u32[]{:S(2)}) copy-start(s32[32]{0:T(128)} %param.7) | copy-start | bytes 388
  54.2 27.8 %collective-permute-start.2 = (f32[8,2,2,4,3,256]{5,0,4,3,1,2:T(8,128)S(1)}, f32[8,2,2,4,3,256]{5,0,4,3,1,2:T(8,128)S(1)}, u32[]{:S(2)}, u32[]{:S(2)}) collective-permute-start(f32[8,2,2,4,3,256]{5,0,4,3,1,2:T(8,128)S(1)} %get-tuple-element.11), channel_id=1, source_target_pairs={{0,12},{4,8},{8,4},{12,0},{1,13},{5,9},{9,5},{13,1},{2,14},{6,10},... | collective-permute-start | bytes 1179656 | tf_op jit(solution)/shard_map/ppermute | solution.py:39
Sparse Core Ops, SparseCore 0:
  88.1 16.5 reduce-scatter.3
